TPU v7x, 32 devices: a whole 2x2x4 slice. The times are simulated.
32 devices in a mesh: dp: 8 (over y, x, core), mp: 4 (over z).
Axes of the slice: x: 2, y: 2, z: 4, core: 2. Of those that a mesh axis runs over, the one named last changes fastest.
Arguments:
- tokens: bfloat16 [6144, 6144], P('dp', 'mp'), may hold values from -6 to 6
- ln_gain: bfloat16 [6144], P('mp'), may hold values from 0.5 to 1.5
- weights: bfloat16 [6144, 12288], P('dp', 'mp'), may hold values from -0.078125 to 0.078125
- grad_partials: bfloat16 [8, 6144, 12288], P('dp', None, 'mp'), may hold values from -40 to 40, as said below
Outputs:
- hidden: bfloat16 [6144, 12288], P('dp', 'mp')
- perturbed_weights: bfloat16 [6144, 12288], P('dp', 'mp')
Inputs may be any that keep to these rules, and one draw needn't show every extreme that they name: `grad_partials`: each slice along the first dimension is one data shard's gradient.
All inputs are finite; a program needn't handle non-finite values.
Results may differ from a plain program's by a relative error of at most 0.012.
Values may be sent and summed in bfloat16 or wider, within the bound.
A program may use at most 192 MiB of HBM per device.

v0:
```python
import math

import jax
import jax.numpy as jnp
from jax import lax
from jax.sharding import PartitionSpec as P

FF = 12288


def per_device(tokens, ln_gain, weights, grad_partials):
    feats, gains = (
        lax.all_gather(tokens, "mp", axis=1, tiled=True),
        lax.all_gather(ln_gain, "mp", axis=0, tiled=True),
    )
    values = feats.astype(jnp.float32)
    center = jnp.mean(values, axis=1, keepdims=True)
    spread = jnp.mean((values - center) ** 2, axis=1, keepdims=True)
    normed = ((values - center) / jnp.sqrt(spread + 1e-06) * gains.astype(jnp.float32)).astype(
        jnp.bfloat16
    )
    radius = 0.7 * math.sqrt(FF)
    grad_rows = lax.psum_scatter(grad_partials, "dp", scatter_dimension=1, tiled=True).astype(
        jnp.float32
    )[0]
    squares = lax.psum(jnp.sum(grad_rows * grad_rows), ("dp", "mp"))
    scale = radius / jnp.sqrt(squares + 1e-12)
    perturbed = (weights.astype(jnp.float32) + scale * grad_rows).astype(jnp.bfloat16)
    pre = jnp.dot(
        normed,
        lax.all_gather(perturbed, "dp", axis=0, tiled=True),
        preferred_element_type=jnp.float32,
    )
    hidden = jax.nn.gelu(pre, approximate=False).astype(jnp.bfloat16)
    return (hidden, perturbed)


def solution(mesh):
    placed = (P("dp", "mp"), P("mp"), P("dp", "mp"), P("dp", None, "mp"))
    return jax.shard_map(
        per_device,
        mesh=mesh,
        in_specs=placed,
        out_specs=(P("dp", "mp"), P("dp", "mp")),
        check_vma=False,
    )
```

profile of v0, /device:TPU:0, one launch (start us, length us, event | category | flops | bytes accessed | tf_op | source)
XLA Modules:
  0.0 539.5 jit_solution(957553367051222841)
XLA Ops:
  8.0 0.0 reduce-scatter.2.cloned.1.call-start
  8.0 0.7 reduce-scatter.2.cloned.1.call-update
  8.7 0.0 all-gather.4.cloned.1.call-start
  8.8 0.5 all-gather.4.cloned.1.call-update
  9.3 0.0 all-gather.6.cloned.1.call-start
  9.4 231.5 %reduce-scatter.2.cloned.1.call-done = bf16[1,768,3072]{2,1,0:T(8,128)(2,1)} async-done(((bf16[1,6144,3072]{2,1,0:T(8,128)(2,1)}), bf16[1,768,3072]{2,1,0:T(8,128)(2,1)}) %reduce-scatter.2.cloned.1.call-update) | async-done | bytes 4718608 | tf_op jit(solution)/shard_map/reduce_scatter | solution.py:23
  240.8 5.4 fusion.7
  246.2 39.5 %psum.7 = f32[]{:T(128)} all-reduce(f32[]{:T(128)} %fusion.7), channel_id=1, replica_groups=mesh['dp'=8,'mp'=4] {'dp','mp'}, use_global_device_ids=true, to_apply=%region_4.0 | all-reduce | flops 1 | bytes 8 | tf_op jit(solution)/shard_map/psum | solution.py:26
  286.4 0.0 copy-start.1
  286.4 8.0 %fusion.10 = bf16[768,3072]{1,0:T(8,128)(2,1)} fusion(bf16[1,768,3072]{2,1,0:T(8,128)(2,1)} %reduce-scatter.2.cloned.1.call-done, bf16[768,3072]{1,0:T(8,128)(2,1)} %param.6, f32[]{:T(128)S(6)} %div.21), kind=kLoop, calls=%fused_computation.14 | loop fusion | flops 11796480 | bytes 14155780 | tf_op jit(solution)/shard_map/convert_element_type | solution.py:28
  294.5 0.0 all-gather.6.cloned.1.call-update
  294.5 0.0 copy-done.1
  294.5 13.2 %all-gather = bf16[4,1,1536]{2,1,0:T(2,128)(2,1)S(1)} all-gather(bf16[1,1,1536]{2,1,0:T(2,128)(2,1)S(1)} %reshape.20), channel_id=1, replica_groups=mesh['dp'=8,'mp'=4] {'mp'}, dimensions={0}, use_global_device_ids=true | all-gather | bytes 15360 | tf_op jit(solution)/shard_map/all_gather | solution.py:14
  307.7 0.0 all-gather.4.cloned.1.call-done
  307.7 0.0 copy-start
  307.7 6.9 %convert_reduce_fusion = f32[768]{0:T(1024)S(1)} fusion(bf16[768,6144]{1,0:T(8,128)(2,1)} %all-gather.4.cloned.1.call-done), kind=kLoop, calls=%fused_computation.1 | loop fusion | flops 9436416 | bytes 9440256 | tf_op jit(solution)/shard_map/reduce_sum | solution.py:17
  314.6 1.2 copy-done
  315.9 2.6 fusion.2
  318.4 156.4 %all-gather.6.cloned.1.call-done = bf16[6144,3072]{1,0:T(8,128)(2,1)} async-done(((bf16[768,3072]{1,0:T(8,128)(2,1)}), bf16[6144,3072]{1,0:T(8,128)(2,1)}) %all-gather.6.cloned.1.call-update) | async-done | bytes 37748752 | tf_op jit(solution)/shard_map/all_gather | solution.py:31
  474.8 57.2 %fusion.13 = bf16[768,3072]{1,0:T(8,128)(2,1)} fusion(bf16[6144,3072]{1,0:T(8,128)(2,1)} %all-gather.6.cloned.1.call-done, bf16[768,6144]{1,0:T(8,128)(2,1)} %all-gather.4.cloned.1.call-done, f32[6144]{0:T(1024)S(1)} %bitcast.9, f32[768]{0:T(1024)S(1)} %add_sqrt_fusion, f32[768]{0:T(1024)S(1)} %broadcast_multiply_fusion), kind=kOutput, calls=%fused_computation.17 | convolution fusion | flops 29167976448 | bytes 51935232 | tf_op jit(solution)/shard_map/dot_general | solution.py:29
  (4 shorter events, 0.0 us)
Async XLA Ops:
  8.0 232.9 %reduce-scatter.2.cloned.1.call-start = ((), (), s32[]{:S(2)}) async-start(), calls=%async_computation.2 | async-start | bytes 42467328 | tf_op jit(solution)/shard_map/reduce_scatter | solution.py:23
  8.7 299.0 %all-gather.4.cloned.1.call-start = ((), (), s32[]{:S(2)}) async-start(), calls=%async_computation.1 | async-start | bytes 11796480 | tf_op jit(solution)/shard_map/all_gather | solution.py:13
  9.3 465.5 %all-gather.6.cloned.1.call-start = ((), (), s32[]{:S(2)}) async-start(), calls=%async_computation.3 | async-start | bytes 42467328 | tf_op jit(solution)/shard_map/all_gather | solution.py:31
  286.4 8.1 %copy-start.1 = (bf16[1536]{0:T(1024)(128)(2,1)S(1)}, bf16[1536]{0:T(1024)(128)(2,1)}, u32[]{:S(2)}) copy-start(bf16[1536]{0:T(1024)(128)(2,1)} %param.5) | copy-start | bytes 9220
  307.7 8.1 %copy-start = (bf16[768,6144]{1,0:T(8,128)(2,1)S(1)}, bf16[768,6144]{1,0:T(8,128)(2,1)}, u32[]{:S(2)}) copy-start(bf16[768,6144]{1,0:T(8,128)(2,1)} %all-gather.4.cloned.1.call-done) | copy-start | bytes 28311556
Sparse Core Ops, SparseCore 0:
  12.4 228.3 reduce-scatter.1
Sparse Core Ops, SparseCore 1:
  10.8 169.3 all-gather.3
  294.6 180.2 all-gather.5
where the time goes:
time: 540 us; the launch traced here: 539 us
  waiting for transfers between devices  389 us (72%)
  matrix products  57.2 us (11%)
  blocking collectives  52.7 us (10%)
  other arithmetic  22.9 us (4%)
  between operations  16.2 us (3%)
    reduce_scatter x1, waiting for transfers between devices, per_device(): lax.psum_scatter(grad_partials, 'dp', scatter_dimension=1, tiled=True)  231 us
    all_gather x1, waiting for transfers between devices, per_device(): lax.all_gather(perturbed, 'dp', axis=0, tiled=True)  156 us
    dot_general x1, matrix products, per_device(): jnp.dot(normed, lax.all_gather(perturbed, 'dp', axis=0, tiled=True), pref...  57.2 us
    psum x1, blocking collectives, per_device(): squares = lax.psum(jnp.sum(grad_rows * grad_rows), ('dp', 'mp'))  39.5 us
    all_gather x1, blocking collectives, per_device(): lax.all_gather(ln_gain, 'mp', axis=0, tiled=True)  13.2 us
  transfers between devices with their start and end apart: 3, of which 2 were waited for; matrix products, arithmetic and copies ran while one was open for 4% of the time, Pallas kernels for 0%

commit v1 on v0

v1 whole, which is shorter than its diff:
```python
import functools
import math

import jax
import jax.numpy as jnp
from jax import lax
from jax.experimental import pallas as pl
from jax.experimental.pallas import tpu as pltpu
from jax.sharding import PartitionSpec as P

SUBS = 6
AHEAD = 2
VMEM_LIMIT = 66 * 1000 * 1000


def power_of_two(n):
    return n & (n - 1) == 0


def chip_at(pos, n):
    if not power_of_two(n):
        return pos
    bits = n.bit_length() - 1
    out = 0
    for b in range(bits):
        out = out + ((pos // 2**b + pos // 2 ** (b + 1)) % 2) * 2**b
    return out


def position_of(chip, n):
    if not power_of_two(n):
        return chip
    bits = n.bit_length() - 1
    above, out = 0, 0
    for b in reversed(range(bits)):
        above = (chip // 2**b + above) % 2
        out = out + above * 2**b
    return out


def ring(n):
    me = lax.axis_index("dp")
    chip, core = me // 2, me % 2
    pos = position_of(chip, n)
    right = chip_at((pos + 1) % n, n) * 2 + core
    left = chip_at((pos + n - 1) % n, n) * 2 + core
    return pos, core, (right, left), chip * 2 + 1 - core


def greet(peers):
    barrier = pltpu.get_barrier_semaphore()
    for axis, peer in peers:
        pl.semaphore_signal(
            barrier, inc=1, device_id={axis: peer}, device_id_type=pl.DeviceIdType.MESH
        )
    pl.semaphore_wait(barrier, len(peers))


def others(axis, size):
    me = lax.axis_index(axis)
    return [(axis, (me + k) % size) for k in range(1, size)]


def remote(src, dst, send, recv, peer, axis="dp"):
    return pltpu.make_async_remote_copy(
        src_ref=src,
        dst_ref=dst,
        send_sem=send,
        recv_sem=recv,
        device_id={axis: peer},
        device_id_type=pl.DeviceIdType.MESH,
    )


def scatter_kernel(
    n, n_mp, radius, g_ref, w_ref, gain_ref, out_ref, gains_ref,
    part, recv, own, grad, sq_ref, stat, sums, gains,
    part_send, part_recv, hop_send, hop_recv, own_sem,
    stat_send, stat_recv, sums_send, sums_recv, gain_send, gain_recv,
):
    pos, core, hops, partner = ring(n)
    rows, half = part.shape[2], part.shape[3]
    sub = rows // SUBS
    total = n * SUBS
    tile = 16
    dp_peers, mp_peers = others("dp", 2 * n), others("mp", n_mp)
    greet(dp_peers + mp_peers)

    def block(t, d, which):
        s, i = t // SUBS, t % SUBS
        target = (pos + n - 1 - s + n) % n if d == 0 else (pos + 1 + s) % n
        start = (chip_at(target, n) * 2 + which) * rows + i * sub
        return g_ref.at[pl.ds(pl.multiple_of(start, tile), sub), pl.ds(d * half, half)]

    def piece(ref, t, d):
        return ref.at[t // SUBS, d, pl.ds(pl.multiple_of((t % SUBS) * sub, tile), sub)]

    def push(t, d):
        at = t * 2 + d
        return remote(
            block(t, d, 1 - core), piece(part, t, d), part_send.at[at], part_recv.at[at], partner
        )

    def load(t, d):
        return pltpu.make_async_copy(block(t, d, core), own.at[t % 2, d], own_sem.at[(t % 2) * 2 + d])

    def hop(t, d, src):
        at = t * 2 + d
        return remote(piece(src, t, d), piece(recv, t, d), hop_send.at[at], hop_recv.at[at], hops[d])

    for d in range(2):
        load(0, d).start()

    @pl.loop(0, SUBS)
    def _(t):
        for d in range(2):
            push(t, d).start()

    place = lax.axis_index("mp")
    fetch = pltpu.make_async_copy(w_ref, out_ref, own_sem.at[4])
    fetch.start()
    gain_copies = [
        remote(gain_ref, gains.at[place], gain_send.at[k], gain_recv.at[k], peer, axis)
        for k, (axis, peer) in enumerate(mp_peers)
    ]
    for copy in gain_copies:
        copy.start()
    gains[place] = gain_ref[...]
    sq_ref[...] = jnp.zeros_like(sq_ref)

    def step(t, first, last):
        @pl.when(t + 1 < total)
        def _():
            for d in range(2):
                load(t + 1, d).start()

        @pl.when(t + SUBS < total)
        def _():
            for d in range(2):
                push(t + SUBS, d).start()

        for d in range(2):
            load(t, d).wait()
            push(t, d).wait_recv()
            if not first:
                hop(t - SUBS, d, recv).wait_recv()
            source = piece(part, t, d)
            came = None if first else piece(recv, t - SUBS, d)
            mine = own.at[t % 2, d]

            @pl.loop(0, sub // tile)
            def _(r):
                at = pl.ds(pl.multiple_of(r * tile, tile), tile)
                value = mine[at, :].astype(jnp.float32) + source[at, :].astype(jnp.float32)
                if not first:
                    value = value + came[at, :].astype(jnp.float32)
                if last:
                    row = pl.multiple_of((t % SUBS) * sub + r * tile, tile)
                    grad[pl.ds(row, tile), d * half : (d + 1) * half] = value
                    squared = value * value
                    sq_ref[...] += squared[:8] + squared[8:]
                elif first:
                    source[at, :] = value.astype(jnp.bfloat16)
                else:
                    came[at, :] = value.astype(jnp.bfloat16)

        if not last:
            for d in range(2):
                at = t * 2 + d
                src = piece(part, t, d) if first else piece(recv, t - SUBS, d)
                remote(src, piece(recv, t, d), hop_send.at[at], hop_recv.at[at], hops[d]).start()

    @pl.loop(0, SUBS)
    def _(t):
        step(t, True, False)

    @pl.loop(SUBS, total - SUBS)
    def _(t):
        step(t, False, False)

    @pl.loop(total - SUBS, total)
    def _(t):
        step(t, False, True)

    folded = sq_ref[:, :128]
    for c in range(1, half // 128):
        folded = folded + sq_ref[:, c * 128 : (c + 1) * 128]
    stat[0] = folded

    @pl.loop(0, total)
    def _(t):
        for d in range(2):
            push(t, d).wait_send()

    @pl.loop(0, total - SUBS)
    def _(t):
        for d in range(2):
            hop(t, d, recv).wait_send()

    def share(slots, peers, send, arrive):
        copies = [
            remote(slots.at[0], slots.at[k + 1], send.at[k], arrive.at[k], peer, axis)
            for k, (axis, peer) in enumerate(peers)
        ]
        for copy in copies:
            copy.start()
        for copy in copies:
            copy.wait()
        return jnp.sum(slots[...], axis=0)

    sums[0] = share(stat, dp_peers, stat_send, stat_recv)
    for copy in gain_copies:
        copy.wait()
    gains_ref[...] = gains[...]
    fetch.wait()
    every = share(sums, mp_peers, sums_send, sums_recv)
    squares = jnp.sum(jnp.sum(every, axis=0, keepdims=True), axis=1, keepdims=True)
    scale = radius / jnp.sqrt(squares + 1e-12)

    @pl.loop(0, rows // tile)
    def _(r):
        at = pl.ds(pl.multiple_of(r * tile, tile), tile)
        value = out_ref[at, :].astype(jnp.float32) + scale * grad[at, :]
        out_ref[at, :] = value.astype(jnp.bfloat16)


def reduce_rows(n, n_mp, radius, grads, weights, gain):
    depth, cols = grads.shape
    rows, half = depth // (2 * n), cols // 2
    sub = rows // SUBS
    dma = pltpu.SemaphoreType.DMA
    return pl.pallas_call(
        functools.partial(scatter_kernel, n, n_mp, radius),
        out_shape=(
            jax.ShapeDtypeStruct((rows, cols), jnp.bfloat16),
            jax.ShapeDtypeStruct((n_mp, *gain.shape), jnp.float32),
        ),
        in_specs=[
            pl.BlockSpec(memory_space=pl.ANY),
            pl.BlockSpec(memory_space=pl.ANY),
            pl.BlockSpec(memory_space=pltpu.VMEM),
        ],
        out_specs=(
            pl.BlockSpec(memory_space=pltpu.VMEM),
            pl.BlockSpec(memory_space=pltpu.VMEM),
        ),
        scratch_shapes=[
            pltpu.VMEM((n, 2, rows, half), jnp.bfloat16),
            pltpu.VMEM((n - 1, 2, rows, half), jnp.bfloat16),
            pltpu.VMEM((2, 2, sub, half), jnp.bfloat16),
            pltpu.VMEM((rows, cols), jnp.float32),
            pltpu.VMEM((8, half), jnp.float32),
            pltpu.VMEM((2 * n, 8, 128), jnp.float32),
            pltpu.VMEM((n_mp, 8, 128), jnp.float32),
            pltpu.VMEM((n_mp, *gain.shape), jnp.float32),
            dma((n * SUBS * 2,)),
            dma((n * SUBS * 2,)),
            dma(((n - 1) * SUBS * 2,)),
            dma(((n - 1) * SUBS * 2,)),
            dma((5,)),
            dma((2 * n - 1,)),
            dma((2 * n - 1,)),
            dma((n_mp - 1,)),
            dma((n_mp - 1,)),
            dma((n_mp - 1,)),
            dma((n_mp - 1,)),
        ],
        compiler_params=pltpu.CompilerParams(
            collective_id=1, has_side_effects=True, vmem_limit_bytes=VMEM_LIMIT
        ),
        cost_estimate=pl.CostEstimate(
            flops=200 * 10**9, bytes_accessed=3 * grads.size, transcendentals=0
        ),
        name="reduce_rows",
    )(grads, weights, gain)


def gather_kernel(
    n, x_ref, gain_ref, p_ref, out_ref, normed, buf, pre_ref,
    hop_send, hop_recv, part_send, part_recv, own_sem, x_sem,
):
    pos, core, hops, partner = ring(n)
    rows, width = buf.shape[3] // 2, buf.shape[4]
    half = SUBS * width
    greet([("dp", peer) for peer in (*hops, partner)])

    def mine(i, d):
        return p_ref.at[:, pl.ds(pl.multiple_of(d * half + i * width, 128), width)]

    def piece(s, i, d, which):
        return buf.at[s, d, i, pl.ds(pl.multiple_of(which * rows, 16), rows)]

    def hop(s, i, d, src):
        at = ((s - 1) * SUBS + i) * 2 + d
        return remote(src, piece(s, i, d, core), hop_send.at[at], hop_recv.at[at], hops[d])

    def push(s, i, d, src):
        at = (s * SUBS + i) * 2 + d
        return remote(src, piece(s, i, d, core), part_send.at[at], part_recv.at[at], partner)

    def pushed(s, i, d):
        at = (s * SUBS + i) * 2 + d
        there = piece(s, i, d, 1 - core)
        return remote(there, there, part_send.at[at], part_recv.at[at], partner)

    def keep(i, d):
        return pltpu.make_async_copy(mine(i, d), piece(0, i, d, core), own_sem.at[i * 2 + d])

    fetch = pltpu.make_async_copy(x_ref, normed, x_sem.at[0])
    fetch.start()
    for i in range(AHEAD):
        for d in range(2):
            hop(1, i, d, mine(i, d)).start()

    @pl.loop(0, SUBS)
    def _(i):
        for d in range(2):
            keep(i, d).start()
            push(0, i, d, mine(i, d)).start()

    pre_ref[...] = jnp.zeros_like(pre_ref)
    fetch.wait()

    @pl.loop(0, normed.shape[0] // 16)
    def _(r):
        at = pl.ds(pl.multiple_of(r * 16, 16), 16)
        values = normed[at, :].astype(jnp.float32)
        center = jnp.mean(values, axis=1, keepdims=True)
        moved = values - center
        spread = jnp.mean(moved * moved, axis=1, keepdims=True)
        scaled = moved * (1.0 / jnp.sqrt(spread + 1e-06)) * gain_ref[...]
        normed[at, :] = scaled.astype(jnp.bfloat16)

    def multiply(s, i):
        for d in range(2):
            pushed(s, i, d).wait_recv()
            owner = (pos + n - s) % n if d == 0 else (pos + s) % n
            cols = pl.ds(pl.multiple_of(chip_at(owner, n) * 2 * rows, 128), 2 * rows)
            out = pl.ds(pl.multiple_of(d * half + i * width, 128), width)
            pre_ref[:, out] += jnp.dot(
                normed[:, cols], buf[s, d, i], preferred_element_type=jnp.float32
            )

    def activate(i):
        tall = 64
        for d in range(2):
            cols = pl.ds(pl.multiple_of(d * half + i * width, 128), width)

            @pl.loop(0, pre_ref.shape[0] // tall)
            def _(r):
                at = pl.ds(pl.multiple_of(r * tall, tall), tall)
                pre = pre_ref[at, cols]
                value = 0.5 * pre * (1.0 + lax.erf(pre * math.sqrt(0.5)))
                out_ref[at, cols] = value.astype(jnp.bfloat16)

    @pl.loop(0, SUBS + n - 1)
    def _(wave):
        @pl.when(wave + AHEAD < SUBS)
        def _():
            for d in range(2):
                hop(1, wave + AHEAD, d, mine(wave + AHEAD, d)).start()

        for s in range(1, n):
            i = wave - (s - 1)

            @pl.when((i >= 0) & (i < SUBS))
            def _():
                for d in range(2):
                    hop(s, i, d, piece(s, i, d, core)).wait_recv()
                    if s < n - 1:
                        hop(s + 1, i, d, piece(s, i, d, core)).start()
                    push(s, i, d, piece(s, i, d, core)).start()

            if s == 1:

                @pl.when(wave < SUBS)
                def _():
                    for d in range(2):
                        keep(wave, d).wait()
                    multiply(0, wave)

            @pl.when((i >= 1) & (i <= SUBS))
            def _():
                multiply(s, i - 1)
                if s == n - 1:
                    activate(i - 1)

    @pl.loop(0, SUBS)
    def _(i):
        for d in range(2):
            for s in range(n):
                push(s, i, d, piece(s, i, d, core)).wait_send()
            for s in range(1, n):
                hop(s, i, d, piece(s, i, d, core)).wait_send()


def gather_matmul(n, feats, gains, perturbed):
    tokens, depth = feats.shape
    rows, cols = perturbed.shape
    half = cols // 2
    dma = pltpu.SemaphoreType.DMA
    return pl.pallas_call(
        functools.partial(gather_kernel, n),
        out_shape=jax.ShapeDtypeStruct((tokens, cols), jnp.bfloat16),
        in_specs=[
            pl.BlockSpec(memory_space=pl.ANY),
            pl.BlockSpec(memory_space=pltpu.VMEM),
            pl.BlockSpec(memory_space=pl.ANY),
        ],
        out_specs=pl.BlockSpec(memory_space=pltpu.VMEM),
        scratch_shapes=[
            pltpu.VMEM((tokens, depth), jnp.bfloat16),
            pltpu.VMEM((n, 2, SUBS, 2 * rows, half // SUBS), jnp.bfloat16),
            pltpu.VMEM((tokens, cols), jnp.float32),
            dma(((n - 1) * SUBS * 2,)),
            dma(((n - 1) * SUBS * 2,)),
            dma((n * SUBS * 2,)),
            dma((n * SUBS * 2,)),
            dma((SUBS * 2,)),
            dma((1,)),
        ],
        compiler_params=pltpu.CompilerParams(
            collective_id=2, has_side_effects=True, vmem_limit_bytes=VMEM_LIMIT
        ),
        cost_estimate=pl.CostEstimate(
            flops=2 * tokens * depth * cols,
            bytes_accessed=2 * depth * cols,
            transcendentals=0,
        ),
        name="gather_matmul",
    )(feats, gains, perturbed)


def per_device(n, n_mp, width, tokens, ln_gain, weights, grad_partials):
    feats = lax.all_gather(tokens, "mp", axis=1, tiled=True)
    gain = jnp.broadcast_to(ln_gain.astype(jnp.float32), (8, ln_gain.shape[0]))
    radius = 0.7 * math.sqrt(width)
    perturbed, gains = reduce_rows(n, n_mp, radius, grad_partials[0], weights, gain)
    hidden = gather_matmul(n, feats, gains[:, 0].reshape(1, -1), perturbed)
    return (hidden, perturbed)


def solution(mesh):
    placed = (P("dp", "mp"), P("mp"), P("dp", "mp"), P("dp", None, "mp"))

    def whole(tokens, ln_gain, weights, grad_partials):
        return jax.shard_map(
            functools.partial(per_device, mesh.shape["dp"] // 2, mesh.shape["mp"], weights.shape[1]),
            mesh=mesh,
            in_specs=placed,
            out_specs=(P("dp", "mp"), P("dp", "mp")),
            check_vma=False,
        )(tokens, ln_gain, weights, grad_partials)

    return whole
```

time: 540 us -> 369 us (0.68)
  waiting for transfers between devices: 389 us -> 0.68 us
  Pallas kernels: 0 us -> 344 us
  matrix products: 57.2 us -> 0 us
  blocking collectives: 52.7 us -> 0 us
  other arithmetic: 22.9 us -> 0 us
  local copies, waits for them, and re-layouts: 1.25 us -> 10.1 us
    pallas_call x0 -> x2, Pallas kernels: none -> 344 us  [the longest x1 175 us: reduce_rows(): pl.pallas_call(functools.partial(scatter_kernel, n, n_mp, radius), out_sh...]
    reduce_scatter x1 -> x0, waiting for transfers between devices: 231 us -> none  [per_device(): lax.psum_scatter(grad_partials, 'dp', scatter_dimension=1, tiled=True)]
    all_gather x2 -> x1, waiting for transfers between devices: 156 us -> 0.01 us  [per_device(): feats = lax.all_gather(tokens, 'mp', axis=1, tiled=True)]
    dot_general x1 -> x0, matrix products: 57.2 us -> none  [per_device(): jnp.dot(normed, lax.all_gather(perturbed, 'dp', axis=0, tiled=True), pref...]
    psum x1 -> x0, blocking collectives: 39.5 us -> none  [per_device(): squares = lax.psum(jnp.sum(grad_rows * grad_rows), ('dp', 'mp'))]
    reduce_sum x3 -> x0, other arithmetic: 14.8 us -> none  [the longest x1 6.86 us: per_device(): center = jnp.mean(values, axis=1, keepdims=True)]
    all_gather x1 -> x0, blocking collectives: 13.2 us -> none  [per_device(): lax.all_gather(ln_gain, 'mp', axis=0, tiled=True)]
    convert_element_type x2 -> x0, other arithmetic: 8.06 us -> none  [the longest x1 8.03 us: per_device(): (weights.astype(jnp.float32) + scale * grad_rows).astype(jnp.bfloat16)]
  transfers between devices with their start and end apart: 3 -> 1, of which waited for: 2 -> 0; matrix products, arithmetic and copies ran while one was open for 4% -> 1% of each run, Pallas kernels for 0% -> 48%
where the time goes in v1:
time: 369 us; the launch traced here: 368 us
  Pallas kernels  344 us (93%)
  between operations  14.1 us (4%)
  local copies, waits for them, and re-layouts  10.1 us (3%)
    pallas_call x1, Pallas kernels, reduce_rows(): pl.pallas_call(functools.partial(scatter_kernel, n, n_mp, radius), out_sh...  175 us
    pallas_call x1, Pallas kernels, gather_matmul(): pl.pallas_call(functools.partial(gather_kernel, n), out_shape=jax.ShapeDt...  168 us
  transfers between devices with their start and end apart: 1, of which 0 were waited for; matrix products, arithmetic and copies ran while one was open for 1% of the time, Pallas kernels for 48%

profile of v1, /device:TPU:0, one launch (start us, length us, event | category | flops | bytes accessed | tf_op | source)
XLA Modules:
  0.0 368.4 jit_solution(2411935746292952932)
XLA Ops:
  7.2 0.0 all-gather.2.cloned.1.call-start
  7.2 0.7 all-gather.2.cloned.1.call-update
  7.9 1.3 broadcast_in_dim.3.gain_ref
  9.2 175.2 %reduce_rows.1 = (bf16[768,3072]{1,0:T(8,128)(2,1)}, f32[4,8,1536]{2,1,0:T(8,128)}) custom-call(bf16[6144,3072]{1,0:T(8,128)(2,1)} %bitcast.3, bf16[768,3072]{1,0:T(8,128)(2,1)} %w_ref.1, f32[8,1536]{1,0:T(8,128)} %broadcast_in_dim.3.gain_ref), custom_call_target="tpu_custom_call" | custom-call | flops 199999995904 | bytes 56623104 | tf_op jit(solution)/shard_map/reduce_rows/pallas_call | solution.py:232
  184.5 1.5 slice.3
  186.0 0.0 all-gather.2.cloned.1.call-done.x_ref
  186.0 168.3 %gather_matmul.1 = bf16[768,3072]{1,0:T(8,128)(2,1)} custom-call(bf16[768,6144]{1,0:T(8,128)(2,1)} %all-gather.2.cloned.1.call-done.x_ref, f32[1,6144]{1,0:T(1,128)} %bitcast.2, bf16[768,3072]{1,0:T(8,128)(2,1)} %get-tuple-element.9.p_ref), custom_call_target="tpu_custom_call" | custom-call | flops 28991029248 | bytes 37748736 | tf_op jit(solution)/shard_map/gather_matmul/pallas_call | solution.py:402
  354.3 0.0 copy-start
  354.3 5.0 %copy.8 = bf16[768,3072]{1,0:T(8,128)(2,1)} copy(bf16[768,3072]{1,0:T(8,128)(2,1)} %gather_matmul.1) | data formatting | bytes 9437184
  359.3 0.0 copy-done
  359.3 2.2 copy.9
Async XLA Ops:
  7.2 178.8 %all-gather.2.cloned.1.call-start = ((), (), s32[]{:S(2)}) async-start(), calls=%async_computation | async-start | bytes 11796480 | tf_op jit(solution)/shard_map/all_gather | solution.py:435
  354.3 5.0 %copy-start = (bf16[768,3072]{1,0:T(8,128)(2,1)S(1)}, bf16[768,3072]{1,0:T(8,128)(2,1)}, u32[]{:S(2)}) copy-start(bf16[768,3072]{1,0:T(8,128)(2,1)} %get-tuple-element.9.p_ref) | copy-start | bytes 14155780
Sparse Core Ops, SparseCore 0:
  9.5 169.7 all-gather.1
